TPU v7x, 32 devices: a whole 2x2x4 slice. The times are simulated.
32 devices in a mesh: dp: 2 (over core), tensor: 16 (over z, y, x).
Axes of the slice: x: 2, y: 2, z: 4, core: 2. Of those that a mesh axis runs over, the one named last changes fastest.
Arguments:
- gradient: float32 [2, 8192, 512], P('dp', 'tensor'), may hold values from -80 to 80
Outputs:
- update: bfloat16 [2, 8192, 512], P(None, 'tensor')
All inputs are finite; a program needn't handle non-finite values.
Results may differ from a plain program's by a relative error of at most 0.001.
Values may be sent and summed in bfloat16 or wider, within the bound.
A program may use at most 64 MiB of HBM per device.

v0:
```python
import math

import jax
import jax.numpy as jnp
from jax import lax
from jax.sharding import PartitionSpec as P

FEATURES = 8192
OUTPUTS = 512
ITERS = 3


linear_term = 3.4445
cubic_term = -4.775
quintic_term = 2.0315
norm_floor = 1e-07
update_gain = 0.2


def multiply(first_factor, second_factor):
    return jnp.einsum("mrs,mst->mrt", first_factor, second_factor, precision=lax.Precision.HIGHEST)


def local_gram(gradient):
    return jnp.einsum("mfr,mfs->mrs", gradient, gradient, precision=lax.Precision.HIGHEST)


def reduce_gram(partial_gram):
    return lax.psum(partial_gram, "tensor")


def replicated_total(gram_matrix):
    order = gram_matrix.shape[2]
    identity = jnp.eye(order, dtype=jnp.float32)[None]
    running = identity
    for turn_index in range(ITERS):
        squared = multiply(gram_matrix, gram_matrix)
        polynomial = linear_term * identity + cubic_term * gram_matrix + quintic_term * squared
        if turn_index == 0:
            running = polynomial
        else:
            running = multiply(running, polynomial)
        if turn_index + 1 < ITERS:
            gram_matrix = multiply(multiply(polynomial, gram_matrix), polynomial)
    return running


def on_device(gradient):
    summed = reduce_gram(local_gram(gradient))
    squared_norm = lax.psum(jnp.sum(gradient * gradient, axis=(1, 2)), "tensor")
    divisor = jnp.sqrt(squared_norm) + norm_floor
    gram_matrix = summed / (divisor * divisor)[:, None, None]
    polished = jnp.einsum(
        "mfr,mrs->mfs", gradient, replicated_total(gram_matrix), precision=lax.Precision.HIGHEST
    )
    factor = update_gain * math.sqrt(max(FEATURES, OUTPUTS)) / divisor
    update = (factor[:, None, None] * polished).astype(jnp.bfloat16)
    return lax.all_gather(update, "dp", axis=0, tiled=True)


def solution(mesh):
    placed = (P("dp", "tensor", None),)
    return jax.shard_map(
        on_device, mesh=mesh, in_specs=placed, out_specs=P(None, "tensor", None), check_vma=False
    )
```

profile of v0, /device:TPU:0, one launch (start us, length us, event | category | flops | bytes accessed | tf_op | source)
XLA Modules:
  0.0 168.9 jit_solution(15192486878711117701)
XLA Ops:
  6.5 0.0 all-reduce.2.cloned.1.call-start
  6.5 4.6 %convolution_bitcast_fusion = f32[1,512,512]{2,1,0:T(8,128)} fusion(f32[1,512,512]{2,1,0:T(8,128)} %param.1), kind=kOutput, calls=%fused_computation.9 | convolution fusion | flops 1610612736 | bytes 2097152 | tf_op jit(solution)/shard_map/mfr,mfs->mrs/dot_general | solution.py:25
  11.2 0.0 copy-start
  11.2 0.0 all-reduce.2.cloned.1.call-update
  11.2 0.0 all-gather.3.cloned.1.call-start
  11.3 1.1 copy-done
  12.4 0.9 multiply_reduce_fusion
  13.3 44.5 %psum.14 = f32[1]{0:T(128)} all-reduce(f32[1]{0:T(128)} %bitcast), channel_id=1, replica_groups=mesh['dp'=2,'tensor'=16] {'tensor'}, use_global_device_ids=true, to_apply=%region_1.0 | all-reduce | flops 1 | bytes 8 | tf_op jit(solution)/shard_map/psum | solution.py:50
  58.5 69.5 %all-reduce.2.cloned.1.call-done = f32[1,512,512]{2,1,0:T(8,128)} async-done(((f32[1,512,512]{2,1,0:T(8,128)}), f32[1,512,512]{2,1,0:T(8,128)}) %all-reduce.2.cloned.1.call-update) | async-done | bytes 1048592 | tf_op jit(solution)/shard_map/psum | solution.py:29
  128.0 0.0 copy-start.1
  128.0 4.1 %fusion.4 = f32[512,512]{1,0:T(8,128)S(1)} fusion(f32[1,512,512]{2,1,0:T(8,128)} %all-reduce.2.cloned.1.call-done, f32[]{:T(128)} %bitcast.4), kind=kOutput, calls=%fused_computation.11 | convolution fusion | flops 1612709888 | bytes 2097156 | tf_op jit(solution)/shard_map/mrs,mst->mrt/dot_general | solution.py:21
  132.1 0.0 copy-done.1
  132.1 1.9 %fusion.7 = f32[512,512]{1,0:T(8,128)S(1)} fusion(f32[512,512]{1,0:T(8,128)S(1)} %fusion.4, f32[1,512,512]{2,1,0:T(8,128)S(1)} %copy-done.1, f32[]{:T(128)} %bitcast.4), kind=kOutput, calls=%fused_computation.14 | convolution fusion | flops 1610874880 | bytes 3145732 | tf_op jit(solution)/shard_map/mrs,mst->mrt/dot_general | solution.py:21
  133.9 1.8 %fusion.12 = f32[512,512]{1,0:T(8,128)S(1)} fusion(f32[512,512]{1,0:T(8,128)S(1)} %fusion.7, f32[512,512]{1,0:T(8,128)S(1)} %fusion.4), kind=kOutput, calls=%fused_computation.23 | convolution fusion | flops 1610612736 | bytes 3145728 | tf_op jit(solution)/shard_map/mrs,mst->mrt/dot_general | solution.py:21
  135.8 1.9 %fusion.1 = f32[512,512]{1,0:T(8,128)S(1)} fusion(f32[512,512]{1,0:T(8,128)S(1)} %fusion.12), kind=kOutput, calls=%fused_computation.6 | convolution fusion | flops 1612185600 | bytes 2097152 | tf_op jit(solution)/shard_map/mrs,mst->mrt/dot_general | solution.py:21
  137.7 1.8 %fusion.14 = f32[512,512]{1,0:T(8,128)S(1)} fusion(f32[512,512]{1,0:T(8,128)S(1)} %fusion.1, f32[512,512]{1,0:T(8,128)S(1)} %fusion.12), kind=kOutput, calls=%fused_computation.25 | convolution fusion | flops 1610612736 | bytes 3145728 | tf_op jit(solution)/shard_map/mrs,mst->mrt/dot_general | solution.py:21
  139.6 1.8 %fusion.13 = f32[512,512]{1,0:T(8,128)S(1)} fusion(f32[512,512]{1,0:T(8,128)S(1)} %fusion.4, f32[512,512]{1,0:T(8,128)S(1)} %fusion.1), kind=kOutput, calls=%fused_computation.24 | convolution fusion | flops 1610612736 | bytes 3145728 | tf_op jit(solution)/shard_map/mrs,mst->mrt/dot_general | solution.py:21
  141.4 2.1 %fusion.15 = f32[512,512]{1,0:T(8,128)S(1)} fusion(f32[512,512]{1,0:T(8,128)S(1)} %fusion.14, f32[512,512]{1,0:T(8,128)S(1)} %fusion.1), kind=kOutput, calls=%fused_computation.26 | convolution fusion | flops 1610612736 | bytes 3145728 | tf_op jit(solution)/shard_map/mrs,mst->mrt/dot_general | solution.py:21
  143.5 1.9 %fusion = f32[512,512]{1,0:T(8,128)S(1)} fusion(f32[512,512]{1,0:T(8,128)S(1)} %fusion.15), kind=kOutput, calls=%fused_computation.4 | convolution fusion | flops 1612185600 | bytes 2097152 | tf_op jit(solution)/shard_map/mrs,mst->mrt/dot_general | solution.py:21
  145.4 1.8 %fusion.16 = f32[512,512]{1,0:T(8,128)S(1)} fusion(f32[512,512]{1,0:T(8,128)S(1)} %fusion.13, f32[512,512]{1,0:T(8,128)S(1)} %fusion), kind=kOutput, calls=%fused_computation.27 | convolution fusion | flops 1610612736 | bytes 3145728 | tf_op jit(solution)/shard_map/mrs,mst->mrt/dot_general | solution.py:21
  147.3 4.3 %fusion.6 = bf16[512,512]{0,1:T(8,128)(2,1)} fusion(f32[512,512]{1,0:T(8,128)S(1)} %fusion.16, f32[1,512,512]{2,1,0:T(8,128)S(1)} %copy-done, f32[]{:T(128)} %bitcast.1), kind=kOutput, calls=%fused_computation.13 | convolution fusion | flops 1611137024 | bytes 2621444 | tf_op jit(solution)/shard_map/mfr,mrs->mfs/dot_general | solution.py:53
  151.5 0.0 all-gather.3.cloned.1.call-update
  151.6 8.3 %all-gather.3.cloned.1.call-done = bf16[1024,512]{0,1:T(8,128)(2,1)} async-done(((bf16[512,512]{0,1:T(8,128)(2,1)}), bf16[1024,512]{0,1:T(8,128)(2,1)}) %all-gather.3.cloned.1.call-update) | async-done | bytes 1048592 | tf_op jit(solution)/shard_map/all_gather | solution.py:58
  159.8 2.3 %copy.3 = bf16[1024,512]{1,0:T(8,128)(2,1)} copy(bf16[1024,512]{0,1:T(8,128)(2,1)} %all-gather.3.cloned.1.call-done) | data formatting | bytes 2097152 | tf_op jit(solution)/shard_map/all_gather | solution.py:58
Async XLA Ops:
  6.5 121.5 %all-reduce.2.cloned.1.call-start = ((), (), s32[]{:S(2)}) async-start(), calls=%async_computation | async-start | bytes 2097152 | tf_op jit(solution)/shard_map/psum | solution.py:29
  11.2 1.2 copy-start
  11.2 148.6 %all-gather.3.cloned.1.call-start = ((), (), s32[]{:S(2)}) async-start(), calls=%async_computation.1 | async-start | bytes 1572864 | tf_op jit(solution)/shard_map/all_gather | solution.py:58
  128.0 4.1 %copy-start.1 = (f32[1,512,512]{2,1,0:T(8,128)S(1)}, f32[1,512,512]{2,1,0:T(8,128)}, u32[]{:S(2)}) copy-start(f32[1,512,512]{2,1,0:T(8,128)} %all-reduce.2.cloned.1.call-done) | copy-start | bytes 3145732
Sparse Core Ops, SparseCore 0:
  12.6 115.3 all-reduce.1
  151.7 8.0 all-gather.2
where the time goes:
time: 169 us
  waiting for transfers between devices  77.8 us (46%)
  blocking collectives  44.5 us (26%)
  matrix products  28.1 us (17%)
  between operations  14.1 us (8%)
  local copies, waits for them, and re-layouts  3.43 us (2%)
    psum x1, waiting for transfers between devices, reduce_gram(): return lax.psum(partial_gram, 'tensor')  69.5 us
    psum x1, blocking collectives, on_device(): squared_norm = lax.psum(jnp.sum(gradient * gradient, axis=(1, 2)), 'tensor')  44.5 us
    dot_general x9, matrix products, multiply(): jnp.einsum('mrs,mst->mrt', first_factor, second_factor, precision=lax.Pre...  19.2 us
    all_gather x1, waiting for transfers between devices, on_device(): return lax.all_gather(update, 'dp', axis=0, tiled=True)  8.26 us
    dot_general x1, matrix products, local_gram(): jnp.einsum('mfr,mfs->mrs', gradient, gradient, precision=lax.Precision.HI...  4.64 us
    dot_general x1, matrix products, on_device(): jnp.einsum('mfr,mrs->mfs', gradient, replicated_total(gram_matrix), preci...  4.28 us
  transfers between devices with their start and end apart: 2, of which 2 were waited for; matrix products, arithmetic and copies ran while one was open for 1% of the time, Pallas kernels for 0%

commit v1 on v0

v1 whole, which is shorter than its diff:
```python
import functools
import math

import jax
import jax.numpy as jnp
from jax import lax
from jax.experimental import pallas as pl
from jax.experimental.pallas import tpu as pltpu
from jax.sharding import PartitionSpec as P

ITERS = 3
BLOCK = 128

linear_term = 3.4445
cubic_term = -4.775
quintic_term = 2.0315
norm_floor = 1e-07
update_gain = 0.2

MESH = pl.DeviceIdType.MESH


def block_pairs(order):
    count = order // BLOCK
    return [(i, j) for i in range(count) for j in range(i, count)]


def split(value):
    high = value.astype(jnp.bfloat16)
    return high, (value - high.astype(jnp.float32)).astype(jnp.bfloat16)


def dot(a, b):
    return lax.dot_general(a, b, (((1,), (0,)), ((), ())), preferred_element_type=jnp.float32)


def kernel(
    shape, g_ref, out_ref, gt, raw, part, recv_in, stage, recv_out, full, gram, lhs, gsplit,
    p0s, ps, qs, gs, s1, r1, s2, r2, s3, r3, s4, r4, s5, r5,
):
    ndp, n_in, n_out, rows, order, chunk = shape
    tile = min(256, rows)
    mtile = min(256, order)
    dp = lax.axis_index("dp")
    tensor = lax.axis_index("tensor")
    ti, to = lax.rem(tensor, n_in), lax.div(tensor, n_in)

    def inner(d):
        return lax.rem(ti + d, n_in)

    def outer(e):
        return lax.rem(to + e, n_out)

    def rank(i, o):
        return o * n_in + i

    def span(i, o):
        return pl.ds(pl.multiple_of((i * n_out + o) * chunk, 8), chunk)

    barrier = pltpu.get_barrier_semaphore()
    for d in range(1, n_in):
        pl.semaphore_signal(barrier, inc=1, device_id=(dp, rank(inner(d), to)), device_id_type=MESH)
    for e in range(1, n_out):
        pl.semaphore_signal(barrier, inc=1, device_id=(dp, rank(ti, outer(e))), device_id_type=MESH)
    for d in range(1, ndp):
        pl.semaphore_signal(
            barrier, inc=1, device_id=(lax.rem(dp + d, ndp), tensor), device_id_type=MESH
        )

    def put(ref, at, value):
        high, low = split(value)
        ref[0, at, :] = high
        ref[1, at, :] = low

    for r in range(0, rows, tile):
        put(gsplit, pl.ds(r, tile), g_ref[pl.ds(r, tile), :])
    turned = g_ref[...].T
    high, low = split(turned)
    gt[0] = high
    gt[1] = low
    for r in range(0, order, mtile):
        at = pl.ds(r, mtile)
        raw[at, :] = (
            dot(gt[0, at, :], gsplit[1]) + dot(gt[1, at, :], gsplit[0])
        ) + dot(gt[0, at, :], gsplit[0])

    pairs = block_pairs(order)
    for b, (i, j) in enumerate(pairs):
        part[pl.ds(b * BLOCK, BLOCK), :] = raw[
            pl.ds(i * BLOCK, BLOCK), pl.ds(j * BLOCK, BLOCK)
        ]
    total_rows = part.shape[0]
    if total_rows > len(pairs) * BLOCK:
        pad = total_rows - len(pairs) * BLOCK
        part[pl.ds(len(pairs) * BLOCK, pad), :] = jnp.zeros((pad, BLOCK), jnp.float32)

    pl.semaphore_wait(barrier, (n_in - 1) + (n_out - 1) + (ndp - 1))

    def remote(src, dst, send, recv, device):
        return pltpu.make_async_remote_copy(
            src_ref=src, dst_ref=dst, send_sem=send, recv_sem=recv,
            device_id=device, device_id_type=MESH,
        )

    turns = list(range(1, n_out))[::-1] + [0]
    first = {}
    for e in turns:
        for d in range(1, n_in):
            copy = remote(
                part.at[span(inner(d), outer(e)), :], recv_in.at[d - 1, e],
                s1.at[d - 1, e], r1.at[d - 1, e], (dp, rank(inner(d), to)),
            )
            copy.start()
            first[d, e] = copy
    second = {}
    for e in turns:
        value = part[span(ti, outer(e)), :]
        for d in range(1, n_in):
            first[d, e].wait_recv()
            value = value + recv_in[d - 1, e]
        if e:
            stage[e - 1] = value
            copy = remote(
                stage.at[e - 1], recv_out.at[e - 1], s2.at[e - 1], r2.at[e - 1],
                (dp, rank(ti, outer(e))),
            )
            copy.start()
            second[e] = copy
    for e in range(1, n_out):
        second[e].wait_recv()
        value = value + recv_out[e - 1]
    full[span(ti, to), :] = value

    third, fourth = {}, {}
    mine = full.at[span(ti, to), :]
    for e in turns[:-1]:
        copy = remote(mine, mine, s3.at[e - 1], r3.at[e - 1], (dp, rank(ti, outer(e))))
        copy.start()
        third[e] = copy

    def pass_on(e):
        block = full.at[span(ti, lax.rem(to - e + n_out, n_out)), :]
        for d in range(1, n_in):
            copy = remote(
                block, block, s4.at[d - 1, e], r4.at[d - 1, e], (dp, rank(inner(d), to))
            )
            copy.start()
            fourth[d, e] = copy

    pass_on(0)
    for e in range(1, n_out):
        third[e].wait_recv()
        pass_on(e)
    for e in range(n_out):
        for d in range(1, n_in):
            fourth[d, e].wait_recv()

    here = lax.broadcasted_iota(jnp.int32, (BLOCK, BLOCK), 0)
    there = lax.broadcasted_iota(jnp.int32, (BLOCK, BLOCK), 1)
    squared = jnp.zeros((BLOCK, BLOCK), jnp.float32)
    for b, (i, j) in enumerate(pairs):
        if i == j:
            squared = squared + jnp.where(here == there, full[pl.ds(b * BLOCK, BLOCK), :], 0.0)
    squared_norm = jnp.sum(jnp.sum(squared, axis=1, keepdims=True), axis=0, keepdims=True)
    divisor = jnp.sqrt(squared_norm) + norm_floor
    scale = 1.0 / (divisor * divisor)
    for b, (i, j) in enumerate(pairs):
        value = full[pl.ds(b * BLOCK, BLOCK), :] * scale
        gram[pl.ds(i * BLOCK, BLOCK), pl.ds(j * BLOCK, BLOCK)] = value
        if i != j:
            gram[pl.ds(j * BLOCK, BLOCK), pl.ds(i * BLOCK, BLOCK)] = value.T

    def product(a, b, at):
        return (
            dot(a[0, at, :], b[1]) + dot(a[1, at, :], b[0])
        ) + dot(a[0, at, :], b[0])

    def polynomial(grams, target):
        for r in range(0, order, mtile):
            at = pl.ds(r, mtile)
            row = lax.broadcasted_iota(jnp.int32, (mtile, order), 0) + r
            column = lax.broadcasted_iota(jnp.int32, (mtile, order), 1)
            value = cubic_term * gram[at, :] + quintic_term * product(grams, grams, at)
            put(target, at, value + jnp.where(row == column, linear_term, 0.0))

    def multiply(a, b, target, keep=None):
        for r in range(0, order, mtile):
            at = pl.ds(r, mtile)
            value = product(a, b, at)
            if keep is not None:
                keep[at, :] = value
            put(target, at, value)

    for r in range(0, order, mtile):
        put(gs, pl.ds(r, mtile), gram[pl.ds(r, mtile), :])
    running, spare = p0s, lhs
    for turn in range(ITERS):
        target = running if turn == 0 else ps
        polynomial(gs, target)
        if turn + 1 < ITERS:
            multiply(target, gs, qs)
            multiply(qs, target, gs, gram)
        if turn > 0:
            multiply(running, target, spare)
            running, spare = spare, running

    factor = update_gain * math.sqrt(max(rows * n_in * n_out, order)) / divisor
    last = []
    for k, r in enumerate(range(0, rows, tile)):
        at = pl.ds(r, tile)
        out_ref[dp, at, :] = (product(gsplit, running, at) * factor).astype(jnp.bfloat16)
        block = out_ref.at[dp, at, :]
        for d in range(1, ndp):
            copy = remote(
                block, block, s5.at[d - 1, k], r5.at[d - 1, k], (lax.rem(dp + d, ndp), tensor)
            )
            copy.start()
            last.append(copy)
    for copy in list(first.values()) + list(second.values()) + list(third.values()):
        copy.wait_send()
    for copy in fourth.values():
        copy.wait_send()
    for copy in last:
        copy.wait()


def on_device(ndp, n, gradient):
    rows, order = gradient.shape[1], gradient.shape[2]
    n_in = 4 if n % 4 == 0 else 1
    n_out = n // n_in
    tile = min(256, rows)
    pieces = rows // tile
    packed = len(block_pairs(order)) * BLOCK
    chunk = -(-packed // (8 * n)) * 8
    total = chunk * n
    shape = (ndp, n_in, n_out, rows, order, chunk)
    bf, f32 = jnp.bfloat16, jnp.float32
    inner, outer = max(n_in - 1, 1), max(n_out - 1, 1)
    dma = pltpu.SemaphoreType.DMA
    pair = pltpu.VMEM((2, order, order), bf)
    return pl.pallas_call(
        functools.partial(kernel, shape),
        out_shape=jax.ShapeDtypeStruct((ndp, rows, order), bf),
        in_specs=[pl.BlockSpec(memory_space=pltpu.VMEM)],
        out_specs=pl.BlockSpec(memory_space=pltpu.VMEM),
        scratch_shapes=[
            pltpu.VMEM((2, order, rows), bf),
            pltpu.VMEM((order, order), f32),
            pltpu.VMEM((total, BLOCK), f32),
            pltpu.VMEM((inner, n_out, chunk, BLOCK), f32),
            pltpu.VMEM((outer, chunk, BLOCK), f32),
            pltpu.VMEM((outer, chunk, BLOCK), f32),
            pltpu.VMEM((total, BLOCK), f32),
            pltpu.VMEM((order, order), f32),
            pair,
            pltpu.VMEM((2, rows, order), bf),
            pair,
            pair,
            pair,
            pair,
            dma((inner, n_out)),
            dma((inner, n_out)),
            dma((outer,)),
            dma((outer,)),
            dma((outer,)),
            dma((outer,)),
            dma((inner, n_out)),
            dma((inner, n_out)),
            dma((max(ndp - 1, 1), pieces)),
            dma((max(ndp - 1, 1), pieces)),
        ],
        compiler_params=pltpu.CompilerParams(
            collective_id=0, has_side_effects=True, vmem_limit_bytes=48 * 1024 * 1024
        ),
    )(gradient[0])


def solution(mesh):
    body = functools.partial(on_device, mesh.shape["dp"], mesh.shape["tensor"])
    return jax.shard_map(
        body, mesh=mesh, in_specs=(P("dp", "tensor", None),),
        out_specs=P(None, "tensor", None), check_vma=False,
    )
```

time: 169 us -> 39.7 us (0.23)
  waiting for transfers between devices: 77.8 us -> 0 us
  blocking collectives: 44.5 us -> 0 us
  Pallas kernels: 0 us -> 37.3 us
  matrix products: 28.1 us -> 0 us
  between operations: 14.1 us -> 0.01 us
    psum x1 -> x0, waiting for transfers between devices: 69.5 us -> none  [reduce_gram(): return lax.psum(partial_gram, 'tensor')]
    psum x1 -> x0, blocking collectives: 44.5 us -> none  [on_device(): squared_norm = lax.psum(jnp.sum(gradient * gradient, axis=(1, 2)), 'tensor')]
    pallas_call x0 -> x1, Pallas kernels: none -> 37.3 us  [on_device(): pl.pallas_call(functools.partial(kernel, shape), out_shape=jax.ShapeDtype...]
    dot_general x11 -> x0, matrix products: 28.1 us -> none  [the longest x9 19.2 us: multiply(): jnp.einsum('mrs,mst->mrt', first_factor, second_factor, precision=lax.Pre...]
    all_gather x1 -> x0, waiting for transfers between devices: 8.26 us -> none  [on_device(): return lax.all_gather(update, 'dp', axis=0, tiled=True)]
    all_gather x1 -> x0, local copies, waits for them, and re-layouts: 2.27 us -> none  [on_device(): return lax.all_gather(update, 'dp', axis=0, tiled=True)]
  transfers between devices with their start and end apart: 2 -> 0, of which waited for: 2 -> 0; matrix products, arithmetic and copies ran while one was open for 1% -> 0% of each run, Pallas kernels for 0% -> 0%
where the time goes in v1:
time: 39.7 us; the launch traced here: 39.5 us
  Pallas kernels  37.3 us (94%)
  local copies, waits for them, and re-layouts  2.2 us (6%)
    pallas_call x1, Pallas kernels, on_device(): pl.pallas_call(functools.partial(kernel, shape), out_shape=jax.ShapeDtype...  37.3 us
    unnamed x3, local copies, waits for them, and re-layouts  2.2 us

profile of v1, /device:TPU:0, one launch (start us, length us, event | category | flops | bytes accessed | tf_op | source)
XLA Modules:
  0.0 39.5 jit_solution(2025148420434159916)
XLA Ops:
  0.0 0.0 copy-start
  0.0 1.2 %copy-done = f32[1,512,512]{2,1,0:T(8,128)S(1)} copy-done((f32[1,512,512]{2,1,0:T(8,128)S(1)}, f32[1,512,512]{2,1,0:T(8,128)}, u32[]{:S(2)}) %copy-start) | copy-done | bytes 1048600
  1.2 37.3 %shard_map.17 = bf16[2,512,512]{2,1,0:T(8,128)(2,1)S(1)} custom-call(f32[512,512]{1,0:T(8,128)S(1)} %bitcast.1), custom_call_target="tpu_custom_call" | custom-call | tf_op jit(solution)/shard_map/pallas_call | solution.py:241
  38.5 1.0 %copy.3 = bf16[2,512,512]{2,1,0:T(8,128)(2,1)} copy(bf16[2,512,512]{2,1,0:T(8,128)(2,1)S(1)} %shard_map.17) | data formatting | bytes 2097152
Async XLA Ops:
  0.0 1.2 %copy-start = (f32[1,512,512]{2,1,0:T(8,128)S(1)}, f32[1,512,512]{2,1,0:T(8,128)}, u32[]{:S(2)}) copy-start(f32[1,512,512]{2,1,0:T(8,128)} %param.1) | copy-start | bytes 3145732

commit v2 on v0

v2 whole, which is shorter than its diff:
```python
import functools
import math

import jax
import jax.numpy as jnp
from jax import lax
from jax.experimental import pallas as pl
from jax.experimental.pallas import tpu as pltpu
from jax.sharding import PartitionSpec as P

ITERS = 3
BLOCK = 128
CUT = 4

linear_term = 3.4445
cubic_term = -4.775
quintic_term = 2.0315
norm_floor = 1e-07
update_gain = 0.2

MESH = pl.DeviceIdType.MESH


def split(value):
    high = value.astype(jnp.bfloat16)
    return high, (value - high.astype(jnp.float32)).astype(jnp.bfloat16)


def dot(a, b):
    return lax.dot_general(a, b, (((1,), (0,)), ((), ())), preferred_element_type=jnp.float32)


def kernel(
    shape, g_hbm, out_ref, g_ref, gt, raw, part, full, gram, spare, gsplit, p0s, ps, qs, gs,
    dtile, dgot_in, dgot_out, in_a, hold_a, out_a, in_b, hold_b, out_b,
    gsem, d1, d2, d3, d4, sems_a, sems_b, s5, r5,
):
    ndp, n_in, n_out, rows, order, chunk, cut = shape
    tile = min(256, rows)
    mtile = min(256, order)
    dp = lax.axis_index("dp")
    tensor = lax.axis_index("tensor")
    ti, to = lax.rem(tensor, n_in), lax.div(tensor, n_in)

    def inner(d):
        return dp, to * n_in + lax.rem(ti + d, n_in)

    def outer(e):
        return dp, lax.rem(to + e, n_out) * n_in + ti

    def sibling(d):
        return lax.rem(dp + d, ndp), tensor

    barrier = pltpu.get_barrier_semaphore()
    for d in range(1, n_in):
        pl.semaphore_signal(barrier, inc=1, device_id=inner(d), device_id_type=MESH)
    for e in range(1, n_out):
        pl.semaphore_signal(barrier, inc=1, device_id=outer(e), device_id_type=MESH)
    for d in range(1, ndp):
        pl.semaphore_signal(barrier, inc=1, device_id=sibling(d), device_id_type=MESH)

    def put(ref, at, columns, value):
        high, low = split(value)
        ref[0, at, columns] = high
        ref[1, at, columns] = low

    every = pl.ds(0, order)
    loads = []
    for k, r in enumerate(range(0, rows, tile)):
        at = pl.ds(r, tile)
        copy = pltpu.make_async_copy(g_hbm.at[at, :], g_ref.at[at, :], gsem.at[k])
        copy.start()
        loads.append(copy)
    for k, r in enumerate(range(0, rows, tile)):
        at = pl.ds(r, tile)
        loads[k].wait()
        value = g_ref[at, :]
        put(gsplit, at, every, value)
        put(gt, every, at, value.T)
    for r in range(0, order, mtile):
        at, columns = pl.ds(r, mtile), pl.ds(r, order - r)
        raw[at, columns] = (
            dot(gt[0, at, :], gsplit[1, :, columns]) + dot(gt[1, at, :], gsplit[0, :, columns])
        ) + dot(gt[0, at, :], gsplit[0, :, columns])

    here = lax.broadcasted_iota(jnp.int32, (BLOCK, BLOCK), 0)
    there = lax.broadcasted_iota(jnp.int32, (BLOCK, BLOCK), 1)
    above, diagonal = here <= there, here == there

    def block(i, j):
        return pl.ds(i * BLOCK, BLOCK), pl.ds(j * BLOCK, BLOCK)

    count = order // BLOCK
    pairs = [(i, j) for i in range(count) for j in range(i + 1, count)]
    for b, (i, j) in enumerate(pairs):
        part[block(b, 0)] = raw[block(i, j)]
    dtile[...] = jnp.zeros_like(dtile)
    for m in range(count // 2):
        one, two = raw[block(2 * m, 2 * m)], raw[block(2 * m + 1, 2 * m + 1)]
        part[block(len(pairs) + m, 0)] = jnp.where(above, one, two)
        dtile[0, pl.ds(m, 1), :] = jnp.sum(jnp.where(diagonal, two, 0.0), axis=0, keepdims=True)
    used = (len(pairs) + count // 2) * BLOCK
    if part.shape[0] > used:
        pad = part.shape[0] - used
        part[pl.ds(used, pad), :] = jnp.zeros((pad, BLOCK), jnp.float32)

    pl.semaphore_wait(barrier, (n_in - 1) + (n_out - 1) + (ndp - 1))

    def remote(src, dst, send, recv, device):
        copy = pltpu.make_async_remote_copy(
            src_ref=src, dst_ref=dst, send_sem=send, recv_sem=recv,
            device_id=device, device_id_type=MESH,
        )
        copy.start()
        return copy

    class Path:
        def __init__(self, flip, start, length, bufs, sems):
            self.flip, self.start, self.length = flip, start, length
            self.got, self.hold, self.got2 = bufs
            self.s1, self.r1, self.s2, self.r2, self.s3, self.r3, self.s4, self.r4 = sems
            self.na, self.nb = (n_out, n_in) if flip else (n_in, n_out)
            self.ia, self.ib = (to, ti) if flip else (ti, to)
            self.to_a, self.to_b = (outer, inner) if flip else (inner, outer)
            self.turns = list(range(1, self.nb))[::-1] + [0]
            self.sent = []
            self.first, self.second, self.third, self.fourth = {}, {}, {}, {}

        def at(self, d, e):
            a, b = lax.rem(self.ia + d + self.na, self.na), lax.rem(self.ib + e + self.nb, self.nb)
            i, o = (b, a) if self.flip else (a, b)
            return pl.ds(
                pl.multiple_of((i * n_out + o) * chunk + self.start, 8), self.length
            )

        def begin(self, e):
            for d in range(1, self.na):
                self.first[d, e] = remote(
                    part.at[self.at(d, e), :], self.got.at[d - 1, e],
                    self.s1.at[d - 1, e], self.r1.at[d - 1, e], self.to_a(d),
                )

        def reduce(self, e):
            value = part[self.at(0, e), :]
            for d in range(1, self.na):
                self.first[d, e].wait_recv()
                value = value + self.got[d - 1, e]
            if e:
                self.hold[e - 1] = value
                self.second[e] = remote(
                    self.hold.at[e - 1], self.got2.at[e - 1], self.s2.at[e - 1],
                    self.r2.at[e - 1], self.to_b(e),
                )
            else:
                for e in range(1, self.nb):
                    self.second[e].wait_recv()
                    value = value + self.got2[e - 1]
                full[self.at(0, 0), :] = value
                mine = full.at[self.at(0, 0), :]
                for e in self.turns[:-1]:
                    self.third[e] = remote(
                        mine, mine, self.s3.at[e - 1], self.r3.at[e - 1], self.to_b(e)
                    )
                self.pass_on(0)

        def pass_on(self, e):
            if e:
                self.third[e].wait_recv()
            held = full.at[self.at(0, -e), :]
            for d in range(1, self.na):
                self.fourth[d, e] = remote(
                    held, held, self.s4.at[d - 1, e], self.r4.at[d - 1, e], self.to_a(d)
                )

        def finish(self):
            for copy in self.fourth.values():
                copy.wait_recv()

        def drain(self):
            for copies in (self.first, self.second, self.third, self.fourth):
                for copy in copies.values():
                    copy.wait_send()

    paths = [Path(False, 0, chunk - cut, (in_a, hold_a, out_a), sems_a)]
    if cut:
        paths.append(Path(True, chunk - cut, cut, (in_b, hold_b, out_b), sems_b))

    def together(name, lists):
        for k in range(max(len(turns) for turns in lists)):
            for path, turns in zip(paths, lists):
                if k < len(turns):
                    getattr(path, name)(turns[k])

    small = []
    for d in range(1, n_in):
        small.append(remote(dtile.at[0], dgot_in.at[d - 1], d1.at[d - 1], d2.at[d - 1], inner(d)))
    together("begin", [path.turns for path in paths])
    value = dtile[0]
    for d in range(1, n_in):
        small[d - 1].wait_recv()
        value = value + dgot_in[d - 1]
    dtile[1] = value
    wide = []
    for e in range(1, n_out):
        wide.append(remote(dtile.at[1], dgot_out.at[e - 1], d3.at[e - 1], d4.at[e - 1], outer(e)))
    together("reduce", [path.turns for path in paths])
    for e in range(1, n_out):
        wide[e - 1].wait_recv()
        value = value + dgot_out[e - 1]
    together("pass_on", [range(1, path.nb) for path in paths])
    for path in paths:
        path.finish()

    squared = jnp.zeros((BLOCK, BLOCK), jnp.float32)
    for m in range(count // 2):
        mixed = full[block(len(pairs) + m, 0)]
        squared = squared + jnp.where(diagonal, mixed + value[m : m + 1, :], 0.0)
    squared_norm = jnp.sum(jnp.sum(squared, axis=1, keepdims=True), axis=0, keepdims=True)
    divisor = jnp.sqrt(squared_norm) + norm_floor
    scale = 1.0 / (divisor * divisor)

    def place(i, j, block_value):
        gram[block(i, j)] = block_value
        put(gs, *block(i, j), block_value)

    for b, (i, j) in enumerate(pairs):
        scaled = full[block(b, 0)] * scale
        place(i, j, scaled)
        put(gs, *block(j, i), scaled.T)
        if i // (mtile // BLOCK) == j // (mtile // BLOCK):
            gram[block(j, i)] = scaled.T
    for m in range(count // 2):
        mixed = full[block(len(pairs) + m, 0)] * scale
        turned = mixed.T
        place(2 * m, 2 * m, jnp.where(above, mixed, turned))
        corner = jnp.where(diagonal, value[m : m + 1, :] * scale, turned)
        place(2 * m + 1, 2 * m + 1, jnp.where(here > there, mixed, corner))

    def product(a, b, at, columns):
        return (
            dot(a[0, at, :], b[1, :, columns]) + dot(a[1, at, :], b[0, :, columns])
        ) + dot(a[0, at, :], b[0, :, columns])

    def symmetric(a, b, target, ending):
        for r in range(0, order, mtile):
            at, columns = pl.ds(r, mtile), pl.ds(r, order - r)
            value = ending(r, at, columns, product(a, b, at, columns))
            put(target, at, columns, value)
            for c in range(r + mtile, order, mtile):
                put(target, pl.ds(c, mtile), at, value[:, c - r : c - r + mtile].T)

    def polynomial(r, at, columns, value):
        row = lax.broadcasted_iota(jnp.int32, value.shape, 0)
        column = lax.broadcasted_iota(jnp.int32, value.shape, 1)
        value = cubic_term * gram[at, columns] + quintic_term * value
        return value + jnp.where(row == column, linear_term, 0.0)

    def keep(r, at, columns, value):
        gram[at, columns] = value
        return value

    def plain(r, at, columns, value):
        return value

    running = p0s
    for turn in range(ITERS):
        target = running if turn == 0 else ps
        symmetric(gs, gs, target, polynomial)
        if turn + 1 < ITERS:
            symmetric(target, gs, qs, plain)
            symmetric(qs, target, gs, keep)
        if turn > 0:
            symmetric(running, target, spare, plain)
            running, spare = spare, running

    factor = update_gain * math.sqrt(max(rows * n_in * n_out, order)) / divisor
    last = []
    for c in range(0, order, mtile):
        for r in range(0, rows, tile):
            at, columns = pl.ds(r, tile), pl.ds(c, mtile)
            out_ref[dp, at, columns] = (
                product(gsplit, running, at, columns) * factor
            ).astype(jnp.bfloat16)
            done = out_ref.at[dp, at, columns]
            k = len(last) // max(ndp - 1, 1)
            for d in range(1, ndp):
                last.append(remote(done, done, s5.at[d - 1, k], r5.at[d - 1, k], sibling(d)))
    for path in paths:
        path.drain()
    for copy in small + wide:
        copy.wait_send()
    for copy in last:
        copy.wait()


def on_device(ndp, n, gradient):
    rows, order = gradient.shape[1], gradient.shape[2]
    n_in = 4 if n % 4 == 0 else 1
    n_out = n // n_in
    tile, mtile = min(256, rows), min(256, order)
    pieces = (rows // tile) * (order // mtile)
    count = order // BLOCK
    packed = count * count // 2 * BLOCK
    chunk = -(-packed // (8 * n)) * 8
    cut = chunk // CUT // 8 * 8 if n_in > 1 and n_out > 1 else 0
    total = chunk * n
    shape = (ndp, n_in, n_out, rows, order, chunk, cut)
    bf, f32 = jnp.bfloat16, jnp.float32
    inner, outer = max(n_in - 1, 1), max(n_out - 1, 1)
    dma = pltpu.SemaphoreType.DMA
    pair = pltpu.VMEM((2, order, order), bf)

    def buffers(na, nb, length):
        return [
            pltpu.VMEM((na, nb + 1, length, BLOCK), f32),
            pltpu.VMEM((nb, length, BLOCK), f32),
            pltpu.VMEM((nb, length, BLOCK), f32),
        ]

    def semaphores(na, nb):
        both = dma((na, nb + 1))
        return (both, both) + (dma((nb,)),) * 4 + (both, both)

    return pl.pallas_call(
        functools.partial(kernel, shape),
        out_shape=pltpu.VMEM((ndp, rows, order), bf),
        in_specs=[pl.BlockSpec(memory_space=pltpu.HBM)],
        out_specs=pl.BlockSpec(memory_space=pltpu.VMEM),
        scratch_shapes=[
            pltpu.VMEM((rows, order), f32),
            pltpu.VMEM((2, order, rows), bf),
            pltpu.VMEM((order, order), f32),
            pltpu.VMEM((total, BLOCK), f32),
            pltpu.VMEM((total, BLOCK), f32),
            pltpu.VMEM((order, order), f32),
            pair,
            pltpu.VMEM((2, rows, order), bf),
            pair, pair, pair, pair,
            pltpu.VMEM((2, 8, BLOCK), f32),
            pltpu.VMEM((inner, 8, BLOCK), f32),
            pltpu.VMEM((outer, 8, BLOCK), f32),
            *buffers(inner, outer, chunk - cut),
            *buffers(outer, inner, max(cut, 8)),
            dma((rows // tile,)),
            dma((inner,)), dma((inner,)), dma((outer,)), dma((outer,)),
            semaphores(inner, outer),
            semaphores(outer, inner),
            dma((max(ndp - 1, 1), pieces)),
            dma((max(ndp - 1, 1), pieces)),
        ],
        compiler_params=pltpu.CompilerParams(
            collective_id=0, has_side_effects=True, vmem_limit_bytes=62464 * 1024
        ),
    )(gradient[0])


def solution(mesh):
    body = functools.partial(on_device, mesh.shape["dp"], mesh.shape["tensor"])
    return jax.shard_map(
        body, mesh=mesh, in_specs=(P("dp", "tensor", None),),
        out_specs=P(None, "tensor", None), check_vma=False,
    )
```

time: 169 us -> 35.5 us (0.21)
  waiting for transfers between devices: 77.8 us -> 0 us
  blocking collectives: 44.5 us -> 0 us
  Pallas kernels: 0 us -> 34.4 us
  matrix products: 28.1 us -> 0 us
  between operations: 14.1 us -> 0.01 us
  local copies, waits for them, and re-layouts: 3.43 us -> 0.97 us
    psum x1 -> x0, waiting for transfers between devices: 69.5 us -> none  [reduce_gram(): return lax.psum(partial_gram, 'tensor')]
    psum x1 -> x0, blocking collectives: 44.5 us -> none  [on_device(): squared_norm = lax.psum(jnp.sum(gradient * gradient, axis=(1, 2)), 'tensor')]
    pallas_call x0 -> x1, Pallas kernels: none -> 34.4 us  [on_device(): pl.pallas_call(functools.partial(kernel, shape), out_shape=pltpu.VMEM((nd...]
    dot_general x11 -> x0, matrix products: 28.1 us -> none  [the longest x9 19.2 us: multiply(): jnp.einsum('mrs,mst->mrt', first_factor, second_factor, precision=lax.Pre...]
    all_gather x1 -> x0, waiting for transfers between devices: 8.26 us -> none  [on_device(): return lax.all_gather(update, 'dp', axis=0, tiled=True)]
    all_gather x1 -> x0, local copies, waits for them, and re-layouts: 2.27 us -> none  [on_device(): return lax.all_gather(update, 'dp', axis=0, tiled=True)]
  transfers between devices with their start and end apart: 2 -> 0, of which waited for: 2 -> 0; matrix products, arithmetic and copies ran while one was open for 1% -> 0% of each run, Pallas kernels for 0% -> 0%
where the time goes in v2:
time: 35.5 us; the launch traced here: 35.4 us
  Pallas kernels  34.4 us (97%)
  local copies, waits for them, and re-layouts  0.97 us (3%)
    pallas_call x1, Pallas kernels, on_device(): pl.pallas_call(functools.partial(kernel, shape), out_shape=pltpu.VMEM((nd...  34.4 us
    unnamed x1, local copies, waits for them, and re-layouts  0.97 us

profile of v2, /device:TPU:0, one launch (start us, length us, event | category | flops | bytes accessed | tf_op | source)
XLA Modules:
  0.0 35.4 jit_solution(6510714804100295562)
XLA Ops:
  0.0 34.4 %shard_map.17 = bf16[2,512,512]{2,1,0:T(8,128)(2,1)S(1)} custom-call(f32[512,512]{1,0:T(8,128)} %bitcast.1), custom_call_target="tpu_custom_call" | custom-call | tf_op jit(solution)/shard_map/pallas_call | solution.py:324
  34.4 1.0 %copy.3 = bf16[2,512,512]{2,1,0:T(8,128)(2,1)} copy(bf16[2,512,512]{2,1,0:T(8,128)(2,1)S(1)} %shard_map.17) | data formatting | bytes 2097152
